TPU v7x, 32 devices: a whole 2x2x4 slice. The times are simulated.
32 devices in a mesh: pts: 16 (over z, x, core), grp: 2 (over y).
Axes of the slice: x: 2, y: 2, z: 4, core: 2. Of those that a mesh axis runs over, the one named last changes fastest.
Arguments:
- cam_jac: float32 [2, 9, 219136], P(None, None, ('pts', 'grp')), may hold values from -6 to 6
- pt_jac: float32 [2, 3, 219136], P(None, None, ('pts', 'grp')), may hold values from -6 to 6
- cam_slot: int32 [219136], P(('pts', 'grp')), may hold values from 0 to 127
- obs_point: int32 [219136], P(('pts', 'grp')), may hold values from 0 to 2047
- cam_inverse: float32 [9, 9, 13696], replicated, may hold values from -1 to 1, as said below
- pt_inverse: float32 [3, 3, 65536], P(None, None, ('pts', 'grp')), may hold values from -1 to 1, as said below
- cam_rhs: float32 [9, 13696], replicated, may hold values from -48 to 48
- pt_rhs: float32 [3, 65536], P(None, ('pts', 'grp')), may hold values from -240 to 240
Outputs:
- camera_step: float32 [9, 13696], replicated
- point_step: float32 [3, 65536], P(None, ('pts', 'grp'))
- resid_ratio: float32 [], replicated
Inputs may be any that keep to these rules, and one draw needn't show every extreme that they name: The observations of each device come in 107 runs of 64; run b holds observations of cameras b * 128 to (b + 1) * 128 - 1, and cam_slot is the camera's offset in that run's block. The point of observation o is (o // 6848) * 2048 + obs_point[o]. `cam_inverse`: each camera's 9 x 9 block is symmetric positive definite. `pt_inverse`: each point's 3 x 3 block is symmetric positive definite.
All inputs are finite; a program needn't handle non-finite values.
Results may differ from a plain program's by a relative error of at most 0.00014.
Values sent between devices are 32-bit elements; how exact they have to be, the bound alone decides.
A program may use at most 128 MiB of HBM per device.

v0:
```python
import jax
import jax.numpy as jnp
from jax import lax
from jax.sharding import PartitionSpec as P

CAM_BLK = 128
TERMS = 3


def local(cam_jac, pt_jac, cam_slot, obs_point, cam_inverse, pt_inverse, cam_rhs, pt_rhs):
    obs_count = cam_slot.shape[0]
    cameras = cam_rhs.shape[1]
    blocks = cameras // CAM_BLK
    run_len = obs_count // blocks
    points = pt_rhs.shape[1]
    picker = (
        cam_slot.reshape(blocks, run_len)[:, :, None]
        == jnp.arange(CAM_BLK, dtype=jnp.int32)[None, None, :]
    ).astype(jnp.float32)

    def fetch_cams(camera_vec):
        grouped = camera_vec.reshape(9, blocks, CAM_BLK)
        return jnp.einsum("cbk,bsk->cbs", grouped, picker, precision=lax.Precision.HIGHEST).reshape(
            9, obs_count
        )

    def deposit(pulled):
        grouped = pulled.reshape(9, blocks, run_len)
        return jnp.einsum("cbs,bsk->cbk", grouped, picker, precision=lax.Precision.HIGHEST).reshape(
            9, cameras
        )

    def to_points(camera_vec):
        at_obs = fetch_cams(camera_vec)
        projected = jnp.sum(cam_jac * at_obs[None], axis=1)
        lifted = jnp.sum(pt_jac * projected[:, None], axis=0)
        return jnp.zeros((3, points), jnp.float32).at[:, obs_point].add(lifted)

    def to_cameras(point_vec):
        at_obs = jnp.take(point_vec, obs_point, axis=1)
        projected = jnp.sum(pt_jac * at_obs[None], axis=1)
        pulled = jnp.sum(cam_jac * projected[:, None], axis=0)
        return deposit(pulled)

    def point_solve(point_vec):
        return jnp.sum(pt_inverse * point_vec[None], axis=1)

    def camera_solve(camera_vec, inverse):
        return jnp.sum(inverse * camera_vec[None], axis=1)

    def combine(partial_sum):
        summed = lax.psum(partial_sum, ("pts", "grp"))
        return camera_solve(summed, cam_inverse)

    series_term = camera_solve(cam_rhs, cam_inverse) - combine(to_cameras(point_solve(pt_rhs)))
    camera_step = series_term
    for series_index in range(TERMS):
        series_term = combine(to_cameras(point_solve(to_points(series_term))))
        camera_step = camera_step + series_term
    point_resid = pt_rhs - to_points(camera_step)
    point_step = point_solve(point_resid)
    resid_total, rhs_total = lax.psum(
        (jnp.sum(point_resid * point_resid), jnp.sum(pt_rhs * pt_rhs)), ("pts", "grp")
    )
    return (camera_step, point_step, jnp.sqrt(resid_total / rhs_total))


def solution(mesh):
    placed = (
        P(None, None, ("pts", "grp")),
        P(None, None, ("pts", "grp")),
        P(("pts", "grp")),
        P(("pts", "grp")),
        P(),
        P(None, None, ("pts", "grp")),
        P(),
        P(None, ("pts", "grp")),
    )
    return jax.shard_map(
        local,
        mesh=mesh,
        in_specs=placed,
        out_specs=(P(), P(None, ("pts", "grp")), P()),
        check_vma=False,
    )
```

profile of v0, /device:TPU:0, one launch (start us, length us, event | category | flops | bytes accessed | tf_op | source)
XLA Modules:
  0.0 923.4 jit_solution(16620208784829193962)
XLA Ops:
  10.9 13.5 %gather_fusion = f32[6848,3]{1,0:T(8,128)} fusion(f32[3,2048]{0,1:T(8,128)S(1)} %copy.91, s32[7168]{0:T(1024)S(1)} %pad_clamp_fusion), kind=kCustom, calls=%fused_computation.clone | custom fusion | bytes 191744 | tf_op jit(solution)/shard_map/jit(_take)/gather | solution.py:40
  24.4 6.2 select_bitcast_fusion.3
  30.6 2.6 copy.92
  38.0 132.2 %all-reduce.6.cloned.1.call-done = f32[9,13696]{1,0:T(8,128)} async-done(((f32[9,13696]{1,0:T(8,128)}), f32[9,13696]{1,0:T(8,128)}) %all-reduce.6.cloned.1.call-update) | async-done | bytes 493072 | tf_op jit(solution)/shard_map/psum | solution.py:52
  170.3 6.6 multiply_reduce_fusion.3
  177.0 2.9 fusion.17
  180.8 2.4 copy.97
  183.2 39.8 %scatter_custom_fusion = f32[3,2048]{0,1:T(8,128)S(1)} fusion(s32[6848]{0:T(1024)S(1)} %compare_select_fusion, f32[6848,3]{1,0:T(8,128)} %copy.97, f32[]{:T(128)} %constant.0.clone.1), kind=kCustom, calls=%fused_computation.57 | custom fusion | flops 20544 | bytes 25088 | tf_op jit(solution)/shard_map/scatter-add | solution.py:37
  223.8 13.5 %gather_fusion.1 = f32[6848,3]{1,0:T(8,128)} fusion(f32[3,2048]{0,1:T(8,128)S(1)} %copy.99, s32[7168]{0:T(1024)S(1)} %pad_clamp_fusion), kind=kCustom, calls=%fused_computation.1.clone | custom fusion | bytes 191744 | tf_op jit(solution)/shard_map/jit(_take)/gather | solution.py:40
  237.3 6.2 select_bitcast_fusion.2
  243.5 2.6 copy.100
  250.6 129.2 %all-reduce.8.cloned.1.call-done = f32[9,13696]{1,0:T(8,128)} async-done(((f32[9,13696]{1,0:T(8,128)}), f32[9,13696]{1,0:T(8,128)}) %all-reduce.8.cloned.1.call-update) | async-done | bytes 493072 | tf_op jit(solution)/shard_map/psum | solution.py:52
  379.9 4.9 multiply_reduce_fusion.2
  384.9 2.9 fusion.19
  392.9 39.5 %scatter_custom_fusion.1 = f32[3,2048]{0,1:T(8,128)S(1)} fusion(s32[6848]{0:T(1024)S(1)} %compare_select_fusion, f32[6848,3]{1,0:T(8,128)} %copy.105, f32[]{:T(128)} %constant.0.clone.1), kind=kCustom, calls=%fused_computation.55 | custom fusion | flops 20544 | bytes 25088 | tf_op jit(solution)/shard_map/scatter-add | solution.py:37
  435.4 13.5 %gather_fusion.2 = f32[6848,3]{1,0:T(8,128)} fusion(f32[3,2048]{0,1:T(8,128)S(1)} %copy.107, s32[7168]{0:T(1024)S(1)} %pad_clamp_fusion), kind=kCustom, calls=%fused_computation.2.clone | custom fusion | bytes 191744 | tf_op jit(solution)/shard_map/jit(_take)/gather | solution.py:40
  448.9 6.2 select_bitcast_fusion.1
  455.1 2.6 copy.108
  462.1 129.4 %all-reduce.10.cloned.1.call-done = f32[9,13696]{1,0:T(8,128)} async-done(((f32[9,13696]{1,0:T(8,128)}), f32[9,13696]{1,0:T(8,128)}) %all-reduce.10.cloned.1.call-update) | async-done | bytes 493072 | tf_op jit(solution)/shard_map/psum | solution.py:52
  591.5 4.9 multiply_reduce_fusion.1
  597.3 5.3 fusion.21
  607.8 3.1 copy.113
  611.0 40.2 %scatter_custom_fusion.2 = f32[3,2048]{0,1:T(8,128)} fusion(s32[6848]{0:T(1024)} %copy-done.9, f32[6848,3]{1,0:T(8,128)} %copy.113, f32[]{:T(128)} %constant.0.clone.1), kind=kCustom, calls=%fused_computation.53 | custom fusion | flops 20544 | bytes 25088 | tf_op jit(solution)/shard_map/scatter-add | solution.py:37
  654.2 14.7 %gather_fusion.3 = f32[6848,3]{1,0:T(8,128)} fusion(f32[3,2048]{0,1:T(8,128)} %copy.115, s32[7168]{0:T(1024)S(1)} %pad_clamp_fusion), kind=kCustom, calls=%fused_computation.3.clone | custom fusion | bytes 191744 | tf_op jit(solution)/shard_map/jit(_take)/gather | solution.py:40
  668.9 6.2 select_bitcast_fusion
  675.1 2.6 copy.116
  681.2 4.9 fusion.22
  687.5 129.5 %all-reduce.12.cloned.1.call-done = f32[9,13696]{1,0:T(8,128)} async-done(((f32[9,13696]{1,0:T(8,128)}), f32[9,13696]{1,0:T(8,128)}) %all-reduce.12.cloned.1.call-update) | async-done | bytes 493072 | tf_op jit(solution)/shard_map/psum | solution.py:52
  816.9 4.9 multiply_reduce_fusion
  826.7 2.9 fusion.23
  832.8 39.3 %scatter_custom_fusion.3 = f32[3,2048]{0,1:T(8,128)S(1)} fusion(s32[6848]{0:T(1024)} %copy-done.9, f32[6848,3]{1,0:T(8,128)} %copy.121, f32[]{:T(128)} %constant.0.clone.1), kind=kCustom, calls=%fused_computation.51 | custom fusion | flops 20544 | bytes 25088 | tf_op jit(solution)/shard_map/scatter-add | solution.py:37
  873.9 40.1 %all-reduce = (f32[]{:T(128)}, f32[]{:T(128)}) all-reduce(f32[]{:T(128)} %get-tuple-element.8, f32[]{:T(128)} %get-tuple-element.10), channel_id=1, replica_groups=mesh['pts'=16,'grp'=2] {'pts','grp'}, use_global_device_ids=true, to_apply=%region_35.37 | all-reduce | flops 2 | bytes 16 | tf_op jit(solution)/shard_map/psum | solution.py:62
  (104 shorter events, 50.9 us)
Async XLA Ops:
  7.2 163.1 %all-reduce.6.cloned.1.call-start = ((), (), s32[]{:S(2)}) async-start(), calls=%async_computation | async-start | bytes 1753088 | tf_op jit(solution)/shard_map/psum | solution.py:52
  8.7 384.1 %copy-start.9 = (s32[6848]{0:T(1024)}, s32[6848]{0:T(1024)S(1)}, u32[]{:S(2)}) copy-start(s32[6848]{0:T(1024)S(1)} %compare_select_fusion) | copy-start | bytes 82180
  9.6 375.3 %copy-start.10 = (s32[107,64]{1,0:T(8,128)}, s32[107,64]{1,0:T(8,128)S(1)}, u32[]{:S(2)}) copy-start(s32[107,64]{1,0:T(8,128)S(1)} %eq.15) | copy-start | bytes 82180
  30.6 2.6 copy-start.1
  30.6 2.8 copy-start
  34.2 136.0 %copy-start.7 = (f32[9,13696]{1,0:T(8,128)S(1)}, f32[9,13696]{1,0:T(8,128)}, u32[]{:S(2)}) copy-start(f32[9,13696]{1,0:T(8,128)} %param.16) | copy-start | bytes 1479172
  37.7 342.2 %all-reduce.8.cloned.1.call-start = ((), (), s32[]{:S(2)}) async-start(), calls=%async_computation.1 | async-start | bytes 1753088 | tf_op jit(solution)/shard_map/psum | solution.py:52
  177.0 3.8 copy-start.5
  180.3 43.1 %copy-start.3 = (f32[3,3,2048]{2,1,0:T(4,128)S(1)}, f32[3,3,2048]{2,1,0:T(4,128)}, u32[]{:S(2)}) copy-start(f32[3,3,2048]{2,1,0:T(4,128)} %param.15) | copy-start | bytes 221188
  250.4 341.1 %all-reduce.10.cloned.1.call-start = ((), (), s32[]{:S(2)}) async-start(), calls=%async_computation.2 | async-start | bytes 1753088 | tf_op jit(solution)/shard_map/psum | solution.py:52
  384.9 5.6 copy-start.6
  455.1 3.5 copy-start.11
  462.1 354.9 %all-reduce.12.cloned.1.call-start = ((), (), s32[]{:S(2)}) async-start(), calls=%async_computation.3 | async-start | bytes 1753088 | tf_op jit(solution)/shard_map/psum | solution.py:52
  605.6 47.2 %copy-start.4 = (f32[3,3,2048]{2,1,0:T(4,128)S(1)}, f32[3,3,2048]{2,1,0:T(4,128)}, u32[]{:S(2)}) copy-start(f32[3,3,2048]{2,1,0:T(4,128)} %param.15) | copy-start | bytes 221188
  821.9 0.9 copy-start.2
  822.8 3.9 copy-start.12
  830.0 42.5 %copy-start.8 = (f32[3,2048]{1,0:T(4,128)S(1)}, f32[3,2048]{1,0:T(4,128)}, u32[]{:S(2)}) copy-start(f32[3,2048]{1,0:T(4,128)} %param.17) | copy-start | bytes 73732
Sparse Core Ops, SparseCore 0:
  37.8 132.4 all-reduce.5
  250.5 129.2 all-reduce.7
  462.2 129.2 all-reduce.9
  687.6 129.2 all-reduce.11
where the time goes:
time: 929 us; the launch traced here: 923 us
  waiting for transfers between devices  520 us (56%)
  other arithmetic  222 us (24%)
  local copies, waits for them, and re-layouts  98 us (11%)
  blocking collectives  40.1 us (4%)
  matrix products  24.9 us (3%)
  between operations  17.1 us (2%)
    psum x4, waiting for transfers between devices, combine(): summed = lax.psum(partial_sum, ('pts', 'grp'))  520 us
    scatter-add x4, other arithmetic, to_points(): return jnp.zeros((3, points), jnp.float32).at[:, obs_point].add(lifted)  159 us
    gather x4, local copies, waits for them, and re-layouts, to_cameras(): at_obs = jnp.take(point_vec, obs_point, axis=1)  55.1 us
    psum x1, blocking collectives, local(): lax.psum((jnp.sum(point_resid * point_resid), jnp.sum(pt_rhs * pt_rhs)),...  40.1 us
    select_n x5, other arithmetic, to_cameras(): at_obs = jnp.take(point_vec, obs_point, axis=1)  25.6 us
    reduce_sum x4, other arithmetic, camera_solve(): return jnp.sum(inverse * camera_vec[None], axis=1)  21.4 us
  transfers between devices with their start and end apart: 4, of which 4 were waited for; matrix products, arithmetic and copies ran while one was open for 0% of the time, Pallas kernels for 0%

commit v1 on v0

v1 whole, which is shorter than its diff:
```python
import functools

import jax
import jax.numpy as jnp
from jax import lax
from jax.experimental import pallas as pl
from jax.experimental.pallas import tpu as pltpu
from jax.sharding import PartitionSpec as P

CAM_BLK = 128
TERMS = 3
PER = 4
ROWS = 40
MESH = pl.DeviceIdType.MESH
VMEM = pl.BlockSpec(memory_space=pltpu.VMEM)
F32 = jnp.float32
BF16 = jnp.bfloat16


def halves(v):
    top = v.astype(BF16)
    return top, (v - top.astype(F32)).astype(BF16)


def rows_of(group):
    return pl.ds(16 * (group // 2) + group % 2, 8, stride=2)


def to_points(live, groups, vec, cj, pj, slot, point, quant, left, right):
    lane_low = lax.broadcasted_iota(jnp.int32, (8, 128), 1) < 64
    for group in range(groups):
        u, half = group // 2, group % 2
        rows = rows_of(group)
        index = slot[rows, :]
        proj = [None, None]
        for j in range(9):
            even = vec[pl.ds(8 * u * ROWS + (2 * half) * 9 + j, 8, stride=ROWS), :]
            odd = vec[pl.ds(8 * u * ROWS + (2 * half + 1) * 9 + j, 8, stride=ROWS), :]
            even = jnp.take_along_axis(even, index, axis=1, mode="promise_in_bounds")
            odd = jnp.take_along_axis(odd, index, axis=1, mode="promise_in_bounds")
            got = jnp.where(lane_low, even, odd)
            for a in range(2):
                part = cj[a * 9 + j, rows, :] * got
                proj[a] = part if proj[a] is None else proj[a] + part
        for i in range(3):
            quant[i, rows, :] = pj[i, rows, :] * proj[0] + pj[3 + i, rows, :] * proj[1]
    low = lax.broadcasted_iota(jnp.int32, (128, 128), 0)
    high = lax.broadcasted_iota(jnp.int32, (16, 128), 0)
    for r in range(live):
        cols = slice(r * 128, (r + 1) * 128)
        where = point[r : r + 1, :]
        right[:, cols] = jnp.where(low == (where & 127), 1.0, 0.0).astype(BF16)
        hit = high == (where >> 7)
        for i in range(3):
            v = jnp.where(hit, quant[i, r : r + 1, :], 0.0)
            top, rest = halves(v)
            left[i * 16 : i * 16 + 16, cols] = top
            left[48 + i * 16 : 64 + i * 16, cols] = rest
    both = lax.dot_general(
        left[:, : live * 128], right[:, : live * 128], (((1,), (1,)), ((), ())), preferred_element_type=F32
    )
    return [both[i * 16 : i * 16 + 16] + both[48 + i * 16 : 64 + i * 16] for i in range(3)]


def point_solve(pinv, y):
    return [
        pinv[3 * i] * y[0] + pinv[3 * i + 1] * y[1] + pinv[3 * i + 2] * y[2] for i in range(3)
    ]


def to_cameras(live, groups, z, cj, pj, slot, point, pull, out):
    for group in range(groups):
        rows = rows_of(group)
        where = point[rows, :]
        low, high = where & 127, where >> 7
        got = [jnp.zeros((8, 128), F32)] * 3
        for s in range(16):
            hit = high == s
            for i in range(3):
                row = jnp.broadcast_to(z[i][s : s + 1, :], (8, 128))
                cand = jnp.take_along_axis(row, low, axis=1, mode="promise_in_bounds")
                got[i] = jnp.where(hit, cand, got[i])
        proj = [
            pj[3 * a, rows, :] * got[0] + pj[3 * a + 1, rows, :] * got[1] + pj[3 * a + 2, rows, :] * got[2]
            for a in range(2)
        ]
        for j in range(9):
            pull[pl.ds(64 * j + 16 * (group // 2) + group % 2, 8, stride=2), :] = (
                cj[j, rows, :] * proj[0] + cj[9 + j, rows, :] * proj[1]
            )
    pull[pl.ds(9 * 64, 7 * 64), :] = jnp.zeros((7 * 64, 128), F32)
    lane_low = lax.broadcasted_iota(jnp.int32, (16, 128), 1) < 64
    cams = lax.broadcasted_iota(jnp.int32, (128, 128), 0)
    for r in range(live):
        v = pull[pl.ds(r, 16, stride=64), :]
        e_top, e_rest = halves(jnp.where(lane_low, v, 0.0))
        o_top, o_rest = halves(jnp.where(lane_low, 0.0, v))
        lhs = jnp.concatenate([e_top, e_rest, o_top, o_rest], axis=0)
        hot = jnp.where(cams == slot[r : r + 1, :], 1.0, 0.0).astype(BF16)
        d = lax.dot_general(lhs, hot, (((1,), (1,)), ((), ())), preferred_element_type=F32)
        base = (r // 2) * ROWS + (r % 2) * 18
        out[base : base + 9, :] = (d[0:16] + d[16:32])[0:9]
        out[base + 9 : base + 18, :] = (d[32:48] + d[48:64])[0:9]


def first_body(live, groups, cj, pj, slot, point, pinv, prhs, out, pull):
    z = point_solve(pinv, [prhs[i] for i in range(3)])
    to_cameras(live, groups, z, cj, pj, slot, point, pull, out)


def middle_body(live, groups, vec, cj, pj, slot, point, pinv, out, quant, left, right, pull):
    y = to_points(live, groups, vec, cj, pj, slot, point, quant, left, right)
    z = point_solve(pinv, y)
    to_cameras(live, groups, z, cj, pj, slot, point, pull, out)


def last_body(live, groups, vec, cj, pj, slot, point, pinv, prhs, step, sums, quant, left, right):
    y = to_points(live, groups, vec, cj, pj, slot, point, quant, left, right)
    rhs = [prhs[i] for i in range(3)]
    resid = [rhs[i] - y[i] for i in range(3)]
    z = point_solve(pinv, resid)
    for i in range(3):
        step[i] = z[i]
    for row, vals in ((0, resid), (1, rhs)):
        total = vals[0] * vals[0] + vals[1] * vals[1] + vals[2] * vals[2]
        sums[8 * row : 8 * row + 8, :] = total[0:8] + total[8:16]


def place(grp_size):
    pts, grp = lax.axis_index("pts"), lax.axis_index("grp")
    core = lax.rem(pts, 2)
    chip = (pts // 2) * grp_size + grp

    def at(other):
        return (2 * (other // grp_size) + core, lax.rem(other, grp_size))

    return core, chip, at, (pts + 1 - 2 * core, grp)


def greet(chips, chip, at, twin):
    barrier = pltpu.get_barrier_semaphore()
    pl.semaphore_signal(barrier, inc=1, device_id=twin, device_id_type=MESH)

    def say(k, _):
        pl.semaphore_signal(barrier, inc=1, device_id=at(lax.rem(chip + k, chips)), device_id_type=MESH)
        return 0

    lax.fori_loop(1, chips, say, 0)
    pl.semaphore_wait(barrier, chips)


def combine_body(
    chips, grp_size, chunks, slots, mode, x, inv, base, out, kept,
    twin_buf, mine, inbox, result, a_s, a_r, b_s, b_r, c_s, c_r, d_s, d_r,
):
    core, chip, at, twin = place(grp_size)
    greet(chips, chip, at, twin)

    def owned(c, t):
        return jnp.logical_and(t < slots, c * slots + t < chunks)

    def remote(src, dst, send, recv, device):
        return pltpu.make_async_remote_copy(
            src_ref=src, dst_ref=dst, send_sem=send, recv_sem=recv, device_id=device, device_id_type=MESH
        )

    def loop(start, body):
        def step(k, carry):
            body(k)
            return carry

        lax.fori_loop(start, chips, step, 0)

    def around(k):
        return lax.rem(chip + k, chips)

    def to_twin(t):
        return remote(x.at[1 - core, t], twin_buf.at[t], a_s.at[t], a_r.at[t], twin)

    def to_owner(t):
        return remote(mine.at[t], inbox.at[chip], b_s.at[t], b_r.at[chip], at(t))

    def from_peer(t):
        return remote(mine.at[0], inbox.at[t], b_s.at[0], b_r.at[t], at(t))

    def spread(t):
        return remote(result.at[core, chip], result.at[core, chip], c_s.at[t], c_r.at[chip], at(t))

    def spread_in(t):
        return remote(result.at[core, t], result.at[core, t], c_s.at[0], c_r.at[t], at(t))

    def pass_on(t):
        return remote(result.at[core, t], result.at[core, t], d_s.at[t], d_r.at[t], twin)

    def pass_in(t):
        return remote(result.at[1 - core, t], result.at[1 - core, t], d_s.at[0], d_r.at[t], twin)

    def start_twin(k):
        t = around(k)
        pl.when(owned(1 - core, t))(lambda: to_twin(t).start())

    loop(1, start_twin)
    start_twin(0)

    def reduce_pair(k, send):
        t = around(k)

        @pl.when(owned(core, t))
        def _():
            to_twin(t).wait_recv()
            mine[t] = x[core, t] + twin_buf[t]
            if send:
                to_owner(t).start()

    loop(1, lambda k: reduce_pair(k, True))
    reduce_pair(0, False)

    @pl.when(owned(core, chip))
    def _():
        kept[...] = mine[chip]

        def gather(k):
            t = around(k)
            from_peer(t).wait_recv()
            kept[...] += inbox[t]

        loop(1, gather)
        total = base[...] - kept[...] if mode == 0 else kept[...]
        solved = []
        for b in range(PER):
            piece = None
            for j in range(9):
                term = inv[b, j] * total[9 * b + j : 9 * b + j + 1, :]
                piece = term if piece is None else piece + term
            solved.append(piece)
        solved = jnp.concatenate(solved + [jnp.zeros((ROWS - 9 * PER, 128), F32)], axis=0)
        kept[...] = solved if mode == 0 else solved + base[...]
        result[core, chip] = solved if mode < 2 else solved + base[...]
        loop(1, lambda k: spread(around(k)).start())
        pass_on(chip).start()

    @pl.when(jnp.logical_not(owned(core, chip)))
    def _():
        kept[...] = jnp.zeros((ROWS, 128), F32)

    def forward(k):
        t = around(chips - k)

        @pl.when(owned(core, t))
        def _():
            spread_in(t).wait_recv()
            pass_on(t).start()

    loop(1, forward)

    def finish(k):
        t = around(k)
        pl.when(owned(1 - core, t))(lambda: pass_in(t).wait_recv())

    loop(0, finish)
    for c in range(2):
        for t in range(slots):
            if c * slots + t < chunks:
                out[c, t] = result[c, t]
            else:
                out[c, t] = jnp.zeros((ROWS, 128), F32)

    def drain(k):
        t = around(k)
        pl.when(owned(1 - core, t))(lambda: to_twin(t).wait_send())
        pl.when(owned(core, t))(lambda: pass_on(t).wait_send())

    loop(0, drain)

    def drain_peers(k):
        t = around(k)
        pl.when(owned(core, t))(lambda: to_owner(t).wait_send())
        pl.when(owned(core, chip))(lambda: spread(t).wait_send())

    loop(1, drain_peers)


def ratio_body(chips, grp_size, sums, out, pair, inbox, twin_s, twin_r, b_s, b_r):
    core, chip, at, twin = place(grp_size)
    greet(chips, chip, at, twin)

    def send_twin():
        return pltpu.make_async_remote_copy(
            src_ref=sums, dst_ref=pair, send_sem=twin_s, recv_sem=twin_r, device_id=twin, device_id_type=MESH
        )

    def send(t, slot):
        return pltpu.make_async_remote_copy(
            src_ref=inbox.at[chip], dst_ref=inbox.at[slot], send_sem=b_s.at[t], recv_sem=b_r.at[slot],
            device_id=at(t), device_id_type=MESH,
        )

    send_twin().start()
    send_twin().wait_recv()
    inbox[chip] = sums[...] + pair[...]

    def begin(k, carry):
        send(lax.rem(chip + k, chips), chip).start()
        return carry

    def end(k, carry):
        t = lax.rem(chip + k, chips)
        send(t, t).wait_recv()
        return carry

    def drain(k, carry):
        send(lax.rem(chip + k, chips), chip).wait_send()
        return carry

    lax.fori_loop(1, chips, begin, 0)
    lax.fori_loop(1, chips, end, 0)
    total = inbox[0]
    for t in range(1, chips):
        total = total + inbox[t]
    resid = jnp.sum(total[0:8], keepdims=True)
    rhs = jnp.sum(total[8:16], keepdims=True)
    out[...] = jnp.broadcast_to(jnp.sqrt(resid / rhs), (8, 128))
    lax.fori_loop(1, chips, drain, 0)
    send_twin().wait_send()


def local(pts_size, grp_size, cam_jac, pt_jac, cam_slot, obs_point, cam_inverse, pt_inverse, cam_rhs, pt_rhs):
    obs_count = cam_slot.shape[0]
    cameras = cam_rhs.shape[1]
    blocks = cameras // CAM_BLK
    points = pt_rhs.shape[1]
    chips = pts_size * grp_size // 2
    chunks = -(-blocks // PER)
    slots = -(-chunks // 16) * 8
    assert obs_count == blocks * 64 and slots <= chips and slots == 16 and points == 2048
    width = slots * 2 * 2 * 128
    live = -(-obs_count // 128)
    groups = 2 * (-(-live // 16))
    chunk_cams = PER * CAM_BLK

    def pad_obs(v):
        lead = v.shape[:-1]
        v = jnp.pad(v, [(0, 0)] * len(lead) + [(0, width - obs_count)])
        return v.reshape(-1, width // 128, 128)

    cj, pj = pad_obs(cam_jac), pad_obs(pt_jac)
    slot, point = pad_obs(cam_slot)[0], pad_obs(obs_point)[0]
    pinv = pt_inverse.reshape(9, 16, 128)
    prhs = pt_rhs.reshape(3, 16, 128)

    pts, grp = lax.axis_index("pts"), lax.axis_index("grp")
    chunk = (pts % 2) * slots + (pts // 2) * grp_size + grp
    begin = jnp.minimum(chunk * chunk_cams, cameras)
    edge = jnp.minimum(begin, cameras - chunk_cams)

    def own(v):
        part = lax.dynamic_slice_in_dim(v, edge, chunk_cams, axis=v.ndim - 1)
        part = jnp.pad(part, [(0, 0)] * (v.ndim - 1) + [(0, chunk_cams)])
        part = lax.dynamic_slice_in_dim(part, begin - edge, chunk_cams, axis=v.ndim - 1)
        return part.reshape(v.shape[:-1] + (PER, CAM_BLK))

    inv = jnp.transpose(own(cam_inverse), (2, 1, 0, 3))
    rhs = jnp.transpose(own(cam_rhs), (1, 0, 2)).reshape(PER * 9, 128)
    rhs = jnp.pad(rhs, ((0, ROWS - PER * 9), (0, 0)))

    vec_shape = jax.ShapeDtypeStruct((2 * slots * ROWS, 128), F32)
    quant = pltpu.VMEM((3, width // 128, 128), F32)
    left = pltpu.VMEM((96, width), BF16)
    right = pltpu.VMEM((128, width), BF16)
    pull = pltpu.VMEM((16 * 64, 128), F32)

    first = pl.pallas_call(
        functools.partial(first_body, live, groups),
        out_shape=vec_shape, in_specs=[VMEM] * 6, out_specs=VMEM, scratch_shapes=[pull], name="first",
    )
    middle = pl.pallas_call(
        functools.partial(middle_body, live, groups),
        out_shape=vec_shape, in_specs=[VMEM] * 6, out_specs=VMEM,
        scratch_shapes=[quant, left, right, pull], name="middle",
    )
    last = pl.pallas_call(
        functools.partial(last_body, live, groups),
        out_shape=(jax.ShapeDtypeStruct((3, 16, 128), F32), jax.ShapeDtypeStruct((16, 128), F32)),
        in_specs=[VMEM] * 7, out_specs=(VMEM, VMEM), scratch_shapes=[quant, left, right], name="last",
    )

    def combine(mode, x, base):
        dma = pltpu.SemaphoreType.DMA
        full, kept = pl.pallas_call(
            functools.partial(combine_body, chips, grp_size, chunks, slots, mode),
            out_shape=(
                jax.ShapeDtypeStruct((2, slots, ROWS, 128), F32),
                jax.ShapeDtypeStruct((ROWS, 128), F32),
            ),
            in_specs=[VMEM] * 3, out_specs=(VMEM, VMEM),
            scratch_shapes=[
                pltpu.VMEM((slots, ROWS, 128), F32),
                pltpu.VMEM((slots, ROWS, 128), F32),
                pltpu.VMEM((chips, ROWS, 128), F32),
                pltpu.VMEM((2, slots, ROWS, 128), F32),
                dma((slots,)), dma((slots,)), dma((slots,)), dma((chips,)),
                dma((chips,)), dma((slots,)), dma((slots,)), dma((slots,)),
            ],
            compiler_params=pltpu.CompilerParams(collective_id=mode, has_side_effects=True),
            name=f"combine{mode}",
        )(x.reshape(2, slots, ROWS, 128), inv, base)
        return full.reshape(2 * slots * ROWS, 128), kept

    vec, kept = combine(0, first(cj, pj, slot, point, pinv, prhs), rhs)
    for index in range(TERMS):
        x = middle(vec, cj, pj, slot, point, pinv)
        vec, kept = combine(2 if index == TERMS - 1 else 1, x, kept)
    step, sums = last(vec, cj, pj, slot, point, pinv, prhs)
    dma = pltpu.SemaphoreType.DMA
    ratio = pl.pallas_call(
        functools.partial(ratio_body, chips, grp_size),
        out_shape=jax.ShapeDtypeStruct((8, 128), F32), in_specs=[VMEM], out_specs=VMEM,
        scratch_shapes=[
            pltpu.VMEM((16, 128), F32), pltpu.VMEM((chips, 16, 128), F32),
            dma, dma, dma((chips,)), dma((chips,)),
        ],
        compiler_params=pltpu.CompilerParams(collective_id=3, has_side_effects=True),
        name="ratio",
    )(sums)
    camera_step = vec.reshape(2 * slots, ROWS, 128)[:, : PER * 9].reshape(2 * slots * PER, 9, 128)
    camera_step = jnp.transpose(camera_step[:blocks], (1, 0, 2)).reshape(9, cameras)
    return camera_step, step.reshape(3, points), ratio[0, 0]


def solution(mesh):
    placed = (
        P(None, None, ("pts", "grp")),
        P(None, None, ("pts", "grp")),
        P(("pts", "grp")),
        P(("pts", "grp")),
        P(),
        P(None, None, ("pts", "grp")),
        P(),
        P(None, ("pts", "grp")),
    )
    return jax.shard_map(
        functools.partial(local, mesh.shape["pts"], mesh.shape["grp"]),
        mesh=mesh,
        in_specs=placed,
        out_specs=(P(), P(None, ("pts", "grp")), P()),
        check_vma=False,
    )
```

time: 929 us -> 162 us (0.17)
  waiting for transfers between devices: 520 us -> 0 us
  other arithmetic: 222 us -> 0 us
  Pallas kernels: 0 us -> 144 us
  local copies, waits for them, and re-layouts: 98 us -> 16.4 us
  blocking collectives: 40.1 us -> 0 us
  matrix products: 24.9 us -> 0 us
  between operations: 17.1 us -> 0.81 us
    psum x4 -> x0, waiting for transfers between devices: 520 us -> none  [combine(): summed = lax.psum(partial_sum, ('pts', 'grp'))]
    scatter-add x4 -> x0, other arithmetic: 159 us -> none  [to_points(): return jnp.zeros((3, points), jnp.float32).at[:, obs_point].add(lifted)]
    pallas_call x0 -> x10, Pallas kernels: none -> 144 us  [the longest x4 107 us: combine(): pl.pallas_call(functools.partial(combine_body, chips, grp_size, chunks, s...]
    gather x4 -> x0, local copies, waits for them, and re-layouts: 55.1 us -> none  [to_cameras(): at_obs = jnp.take(point_vec, obs_point, axis=1)]
    psum x1 -> x0, blocking collectives: 40.1 us -> none  [local(): lax.psum((jnp.sum(point_resid * point_resid), jnp.sum(pt_rhs * pt_rhs)),...]
    reduce_sum x26 -> x0, other arithmetic: 34.3 us -> none  [the longest x4 21.4 us: camera_solve(): return jnp.sum(inverse * camera_vec[None], axis=1)]
    select_n x5 -> x0, other arithmetic: 25.6 us -> none  [to_cameras(): at_obs = jnp.take(point_vec, obs_point, axis=1)]
    dot_general x8 -> x0, matrix products: 24.9 us -> none  [the longest x4 14 us: fetch_cams(): jnp.einsum('cbk,bsk->cbs', grouped, picker, precision=lax.Precision.HIGHEST)]
  transfers between devices with their start and end apart: 4 -> 0, of which waited for: 4 -> 0; matrix products, arithmetic and copies ran while one was open for 0% -> 0% of each run, Pallas kernels for 0% -> 0%
where the time goes in v1:
time: 162 us; the launch traced here: 161 us
  Pallas kernels  144 us (89%)
  local copies, waits for them, and re-layouts  16.4 us (10%)
    pallas_call x4, Pallas kernels, combine(): pl.pallas_call(functools.partial(combine_body, chips, grp_size, chunks, s...  107 us
    pallas_call x3, Pallas kernels, local(): x = middle(vec, cj, pj, slot, point, pinv)  15.3 us
    pallas_call x1, Pallas kernels, local(): pl.pallas_call(functools.partial(ratio_body, chips, grp_size), out_shape=...  14.3 us
    unnamed x8, local copies, waits for them, and re-layouts  6.11 us
    pallas_call x1, Pallas kernels, local(): vec, kept = combine(0, first(cj, pj, slot, point, pinv, prhs), rhs)  3.51 us
    pallas_call x1, Pallas kernels, local(): step, sums = last(vec, cj, pj, slot, point, pinv, prhs)  3.44 us

profile of v1, /device:TPU:0, one launch (start us, length us, event | category | flops | bytes accessed | tf_op | source)
XLA Modules:
  0.0 161.1 jit_solution(13646424390272581983)
XLA Ops:
  0.7 1.4 copy.33
  2.1 0.1 constant_dynamic-slice_fusion
  2.2 0.1 pad_dynamic-slice_fusion.1
  2.3 0.6 pad.33.base
  2.9 1.4 pad_bitcast_fusion
  4.3 1.6 reshape.62.pinv
  5.9 1.0 copy.24
  6.9 0.8 reshape.61.pj
  7.7 1.1 constant_dynamic-slice_fusion.1
  8.8 0.1 pad_dynamic-slice_fusion
  9.0 0.1 reshape.65
  9.1 0.8 copy.31
  9.8 1.1 copy.23
  10.9 0.1 pad.27.clone
  11.0 0.9 reshape.60.cj
  11.9 3.5 %first.1 = f32[1280,128]{1,0:T(8,128)} custom-call(f32[18,64,128]{2,1,0:T(8,128)} %reshape.60.cj, f32[6,64,128]{2,1,0:T(8,128)} %reshape.61.pj, s32[64,128]{1,0:T(8,128)} %get-tuple-element.22.slot, s32[64,128]{1,0:T(8,128)} %get-tuple-element.21.point, f32[9,16,128]{2,1,0:T(8,128)} %reshape.62.pinv, f32[3,16,128]{2,1,0:T(8,128)} %bitcast.47), custom_call_target="tpu_custom_call" | custom-call | tf_op jit(solution)/shard_map/first/pallas_call | solution.py:409
  15.4 26.2 %combine0.1 = (f32[2,16,40,128]{3,2,1,0:T(8,128)}, f32[40,128]{1,0:T(8,128)}) custom-call(f32[2,16,40,128]{3,2,1,0:T(8,128)} %bitcast.39, f32[4,9,9,128]{3,2,1,0:T(8,128)} %bitcast.32, f32[40,128]{1,0:T(8,128)} %pad.33.base), custom_call_target="tpu_custom_call" | custom-call | tf_op jit(solution)/shard_map/combine0/pallas_call | solution.py:389
  41.6 5.1 %middle.3 = f32[1280,128]{1,0:T(8,128)} custom-call(f32[1280,128]{1,0:T(8,128)} %bitcast.44, f32[18,64,128]{2,1,0:T(8,128)} %reshape.60.cj, f32[6,64,128]{2,1,0:T(8,128)} %reshape.61.pj, s32[64,128]{1,0:T(8,128)} %get-tuple-element.22.slot, s32[64,128]{1,0:T(8,128)} %get-tuple-element.21.point, f32[9,16,128]{2,1,0:T(8,128)} %reshape.62.pinv), custom_call_target="tpu_custom_call" | custom-call | tf_op jit(solution)/shard_map/middle/pallas_call | solution.py:411
  46.8 27.1 %combine1.2 = (f32[2,16,40,128]{3,2,1,0:T(8,128)}, f32[40,128]{1,0:T(8,128)}) custom-call(f32[2,16,40,128]{3,2,1,0:T(8,128)} %bitcast.41, f32[4,9,9,128]{3,2,1,0:T(8,128)} %bitcast.33, f32[40,128]{1,0:T(8,128)} %get-tuple-element.13.base), custom_call_target="tpu_custom_call" | custom-call | tf_op jit(solution)/shard_map/combine1/pallas_call | solution.py:389
  73.8 5.1 %middle.4 = f32[1280,128]{1,0:T(8,128)} custom-call(f32[1280,128]{1,0:T(8,128)} %bitcast.45, f32[18,64,128]{2,1,0:T(8,128)} %reshape.60.cj, f32[6,64,128]{2,1,0:T(8,128)} %reshape.61.pj, s32[64,128]{1,0:T(8,128)} %get-tuple-element.22.slot, s32[64,128]{1,0:T(8,128)} %get-tuple-element.21.point, f32[9,16,128]{2,1,0:T(8,128)} %reshape.62.pinv), custom_call_target="tpu_custom_call" | custom-call | tf_op jit(solution)/shard_map/middle/pallas_call | solution.py:411
  79.0 27.2 %combine1.3 = (f32[2,16,40,128]{3,2,1,0:T(8,128)}, f32[40,128]{1,0:T(8,128)}) custom-call(f32[2,16,40,128]{3,2,1,0:T(8,128)} %bitcast.42, f32[4,9,9,128]{3,2,1,0:T(8,128)} %bitcast.34, f32[40,128]{1,0:T(8,128)} %get-tuple-element.15.base), custom_call_target="tpu_custom_call" | custom-call | tf_op jit(solution)/shard_map/combine1/pallas_call | solution.py:389
  106.2 5.1 %middle.5 = f32[1280,128]{1,0:T(8,128)} custom-call(f32[1280,128]{1,0:T(8,128)} %bitcast.46, f32[18,64,128]{2,1,0:T(8,128)} %reshape.60.cj, f32[6,64,128]{2,1,0:T(8,128)} %reshape.61.pj, s32[64,128]{1,0:T(8,128)} %get-tuple-element.22.slot, s32[64,128]{1,0:T(8,128)} %get-tuple-element.21.point, f32[9,16,128]{2,1,0:T(8,128)} %reshape.62.pinv), custom_call_target="tpu_custom_call" | custom-call | tf_op jit(solution)/shard_map/middle/pallas_call | solution.py:411
  111.3 26.9 %combine2.1 = (f32[2,16,40,128]{3,2,1,0:T(8,128)}, f32[40,128]{1,0:T(8,128)}) custom-call(f32[2,16,40,128]{3,2,1,0:T(8,128)} %bitcast.40, f32[4,9,9,128]{3,2,1,0:T(8,128)} %bitcast.35, f32[40,128]{1,0:T(8,128)} %get-tuple-element.17.base), custom_call_target="tpu_custom_call" | custom-call | tf_op jit(solution)/shard_map/combine2/pallas_call | solution.py:389
  138.2 3.4 %last.1 = (f32[3,16,128]{2,1,0:T(8,128)}, f32[16,128]{1,0:T(8,128)}) custom-call(f32[1280,128]{1,0:T(8,128)} %bitcast.37, f32[18,64,128]{2,1,0:T(8,128)} %reshape.60.cj, f32[6,64,128]{2,1,0:T(8,128)} %reshape.61.pj, s32[64,128]{1,0:T(8,128)} %get-tuple-element.22.slot, s32[64,128]{1,0:T(8,128)} %get-tuple-element.21.point, f32[9,16,128]{2,1,0:T(8,128)} %reshape.62.pinv, ...), custom_call_target="tpu_custom_call" | custom-call | tf_op jit(solution)/shard_map/last/pallas_call | solution.py:413
  141.7 14.3 %ratio.1 = f32[8,128]{1,0:T(8,128)} custom-call(f32[16,128]{1,0:T(8,128)} %get-tuple-element.20.sums), custom_call_target="tpu_custom_call" | custom-call | tf_op jit(solution)/shard_map/ratio/pallas_call | solution.py:415
  156.0 1.2 slice.11
  157.1 1.4 copy.32
  158.5 1.2 reshape.74
  159.7 0.1 slice_bitcast_fusion
  159.7 0.2 copy.22
  159.9 0.1 pad.34
  160.0 1.2 copy.26
  (6 shorter events, 0.1 us)
Async XLA Ops:
  0.6 1.5 copy-start

commit v2 on v0

v2 whole, which is shorter than its diff:
```python
import functools

import jax
import jax.numpy as jnp
from jax import lax
from jax.experimental import pallas as pl
from jax.experimental.pallas import tpu as pltpu
from jax.sharding import PartitionSpec as P

CAM_BLK = 128
TERMS = 3
PER = 4
ROWS = 40
MESH = pl.DeviceIdType.MESH
VMEM = pl.BlockSpec(memory_space=pltpu.VMEM)
F32 = jnp.float32
BF16 = jnp.bfloat16


def halves(v):
    top = v.astype(BF16)
    return top, (v - top.astype(F32)).astype(BF16)


def rows_of(group):
    return 16 * (group // 2) + group % 2


def prepare(obs, live, cj_in, pj_in, slot, point, pinv_in, prhs_in, cj, pj, pinv, prhs, tail, right, hot):
    for a in range(2):
        for ref, out, count in ((cj_in, cj, 9), (pj_in, pj, 3)):
            for j in range(count):
                begin = live // 8 * 8
                out[(a * count + j) * 64 + begin : (a * count + j + 1) * 64, :] = jnp.zeros((64 - begin, 128), F32)
    tail[...] = jnp.zeros((16, 128), F32)
    for r in range(live):
        span = min(128, obs - r * 128)
        for a in range(2):
            for ref, out, count in ((cj_in, cj, 9), (pj_in, pj, 3)):
                if span == 128:
                    v = ref[a, :, r * 128 : r * 128 + 128]
                else:
                    tail[0:count, 0:span] = ref[a, :, r * 128 : r * 128 + span]
                    v = tail[0:count, :]
                out[pl.ds(a * count * 64 + r, count, stride=64), :] = v
    for s in range(16):
        cols = slice(s * 128, s * 128 + 128)
        prhs[pl.ds(s, 3, stride=16), :] = prhs_in[:, cols]
        for i in range(3):
            pinv[pl.ds(48 * i + s, 3, stride=16), :] = pinv_in[i, :, cols]
    low = lax.broadcasted_iota(jnp.int32, (128, 128), 0)
    for r in range(live):
        cols = slice(r * 128, (r + 1) * 128)
        right[:, cols] = jnp.where(low == (point[r : r + 1, :] & 127), 1.0, 0.0).astype(BF16)
        hot[:, cols] = jnp.where(low == slot[r : r + 1, :], 1.0, 0.0).astype(BF16)


def to_points(live, groups, vec, cj, pj, slot, point, quant, left, right):
    lane_low = lax.broadcasted_iota(jnp.int32, (8, 128), 1) < 64
    for group in range(groups):
        u, half = group // 2, group % 2
        row = rows_of(group)
        index = slot[pl.ds(row, 8, stride=2), :]
        proj = [None, None]
        for j in range(9):
            even = vec[pl.ds(8 * u * ROWS + (2 * half) * 9 + j, 8, stride=ROWS), :]
            odd = vec[pl.ds(8 * u * ROWS + (2 * half + 1) * 9 + j, 8, stride=ROWS), :]
            even = jnp.take_along_axis(even, index, axis=1, mode="promise_in_bounds")
            odd = jnp.take_along_axis(odd, index, axis=1, mode="promise_in_bounds")
            got = jnp.where(lane_low, even, odd)
            for a in range(2):
                part = cj[pl.ds((a * 9 + j) * 64 + row, 8, stride=2), :] * got
                proj[a] = part if proj[a] is None else proj[a] + part
        for i in range(3):
            quant[pl.ds(64 * i + row, 8, stride=2), :] = (
                pj[pl.ds(64 * i + row, 8, stride=2), :] * proj[0]
                + pj[pl.ds(64 * (3 + i) + row, 8, stride=2), :] * proj[1]
            )
    high = lax.broadcasted_iota(jnp.int32, (16, 128), 0)
    for r in range(live):
        cols = slice(r * 128, (r + 1) * 128)
        hit = high == (point[r : r + 1, :] >> 7)
        for i in range(3):
            v = jnp.where(hit, quant[64 * i + r : 64 * i + r + 1, :], 0.0)
            top, rest = halves(v)
            left[i * 16 : i * 16 + 16, cols] = top
            left[48 + i * 16 : 64 + i * 16, cols] = rest
    both = lax.dot_general(left[...], right[...], (((1,), (1,)), ((), ())), preferred_element_type=F32)
    return both[0:48] + both[48:96]


def point_solve(pinv, y):
    out = []
    for i in range(3):
        row = 48 * i
        out.append(
            pinv[row : row + 16] * y[0:16] + pinv[row + 16 : row + 32] * y[16:32] + pinv[row + 32 : row + 48] * y[32:48]
        )
    return jnp.concatenate(out, axis=0)


def to_cameras(live, groups, z, cj, pj, slot, point, hot, pull, out):
    for group in range(groups):
        row = rows_of(group)
        where = point[pl.ds(row, 8, stride=2), :]
        low, high = where & 127, where >> 7
        got = [jnp.zeros((8, 128), F32)] * 3
        for s in range(16):
            hit = high == s
            for i in range(3):
                table = jnp.broadcast_to(z[16 * i + s : 16 * i + s + 1, :], (8, 128))
                cand = jnp.take_along_axis(table, low, axis=1, mode="promise_in_bounds")
                got[i] = jnp.where(hit, cand, got[i])
        proj = []
        for a in range(2):
            part = None
            for i in range(3):
                term = pj[pl.ds((3 * a + i) * 64 + row, 8, stride=2), :] * got[i]
                part = term if part is None else part + term
            proj.append(part)
        for j in range(9):
            pull[pl.ds(64 * j + row, 8, stride=2), :] = (
                cj[pl.ds(64 * j + row, 8, stride=2), :] * proj[0]
                + cj[pl.ds(64 * (9 + j) + row, 8, stride=2), :] * proj[1]
            )
    lane_low = lax.broadcasted_iota(jnp.int32, (16, 128), 1) < 64
    for r in range(live):
        v = pull[pl.ds(r, 16, stride=64), :]
        e_top, e_rest = halves(jnp.where(lane_low, v, 0.0))
        o_top, o_rest = halves(jnp.where(lane_low, 0.0, v))
        lhs = jnp.concatenate([e_top, e_rest, o_top, o_rest], axis=0)
        d = lax.dot_general(
            lhs, hot[:, r * 128 : r * 128 + 128], (((1,), (1,)), ((), ())), preferred_element_type=F32
        )
        base = (r // 2) * ROWS + (r % 2) * 18
        out[base : base + 9, :] = (d[0:16] + d[16:32])[0:9]
        out[base + 9 : base + 18, :] = (d[32:48] + d[48:64])[0:9]


def body(
    chips, grp_size, chunks, slots, blocks, live, groups, obs,
    cj_in, pj_in, slot, point, pinv_in, prhs_in, cinv, crhs,
    cam_out, pt_out, ratio_out,
    cj, pj, pinv, prhs, tail, right, hot, left, quant, pull, zs, x, inv, rhs, kept,
    twin_buf, mine, inbox, result, tile, pair, tiles, left_tiles,
    a_s, a_r, b_s, b_r, c_s, c_r, d_s, d_r, load, p_s, p_r, q_s, q_r,
):
    pts, grp = lax.axis_index("pts"), lax.axis_index("grp")
    core = lax.rem(pts, 2)
    chip = (pts // 2) * grp_size + grp
    twin = (pts + 1 - 2 * core, grp)

    def at(other):
        return (2 * (other // grp_size) + core, lax.rem(other, grp_size))

    def around(k):
        return lax.rem(chip + k, chips)

    def loop(start, step):
        def run(k, carry):
            step(k)
            return carry

        lax.fori_loop(start, chips, run, 0)

    barrier = pltpu.get_barrier_semaphore()
    pl.semaphore_signal(barrier, inc=1, device_id=twin, device_id_type=MESH)
    loop(1, lambda k: pl.semaphore_signal(barrier, inc=1, device_id=at(around(k)), device_id_type=MESH))

    def owned(c, t):
        return jnp.logical_and(t < slots, c * slots + t < chunks)

    def owned_block(b):
        return jnp.logical_and(chip < slots, (core * slots + chip) * PER + b < blocks)

    def loads(b):
        cols = pl.ds(pl.multiple_of(((core * slots + chip) * PER + b) * 128, 128), 128)
        return (
            pltpu.make_async_copy(cinv.at[:, :, cols], inv.at[b], load.at[2 * b]),
            pltpu.make_async_copy(crhs.at[:, cols], rhs.at[b], load.at[2 * b + 1]),
        )

    for b in range(PER):
        @pl.when(owned_block(b))
        def _():
            for copy in loads(b):
                copy.start()

        @pl.when(jnp.logical_not(owned_block(b)))
        def _():
            inv[b] = jnp.zeros((9, 9, 128), F32)
            rhs[b] = jnp.zeros((9, 128), F32)

    prepare(obs, live, cj_in, pj_in, slot, point, pinv_in, prhs_in, cj, pj, pinv, prhs, tail, right, hot)
    x[...] = jnp.zeros_like(x)
    result[...] = jnp.zeros_like(result)
    kept[...] = jnp.zeros_like(kept)
    pull[pl.ds(9 * 64, 7 * 64), :] = jnp.zeros((7 * 64, 128), F32)
    zs[...] = prhs[...]
    for b in range(PER):
        @pl.when(owned_block(b))
        def _():
            for copy in loads(b):
                copy.wait()

    pl.semaphore_wait(barrier, chips)

    def chunk(c, t):
        return pl.ds(pl.multiple_of((c * slots + t) * ROWS, 8), ROWS)

    def remote(src, dst, send, recv, device):
        return pltpu.make_async_remote_copy(
            src_ref=src, dst_ref=dst, send_sem=send, recv_sem=recv, device_id=device, device_id_type=MESH
        )

    def to_twin(t):
        return remote(x.at[chunk(1 - core, t)], twin_buf.at[t], a_s.at[t], a_r.at[t], twin)

    def to_owner(t):
        return remote(mine.at[t], inbox.at[chip], b_s.at[t], b_r.at[chip], at(t))

    def from_peer(t):
        return remote(mine.at[0], inbox.at[t], b_s.at[0], b_r.at[t], at(t))

    def spread(t):
        part = result.at[chunk(core, chip)]
        return remote(part, part, c_s.at[t], c_r.at[chip], at(t))

    def spread_in(t):
        part = result.at[chunk(core, t)]
        return remote(part, part, c_s.at[0], c_r.at[t], at(t))

    def pass_on(t):
        part = result.at[chunk(core, t)]
        return remote(part, part, d_s.at[t], d_r.at[t], twin)

    def pass_in(t):
        part = result.at[chunk(1 - core, t)]
        return remote(part, part, d_s.at[0], d_r.at[t], twin)

    def start_twin(k):
        t = around(k)
        pl.when(owned(1 - core, t))(lambda: to_twin(t).start())

    def reduce_pair(k, send):
        t = around(k)

        @pl.when(owned(core, t))
        def _():
            to_twin(t).wait_recv()
            mine[t] = x[chunk(core, t), :] + twin_buf[t]
            if send:
                to_owner(t).start()

    def forward(k):
        t = around(chips - k)

        @pl.when(owned(core, t))
        def _():
            spread_in(t).wait_recv()
            pass_on(t).start()

    def finish(k):
        t = around(k)
        pl.when(owned(1 - core, t))(lambda: pass_in(t).wait_recv())

    def drain(k):
        t = around(k)
        pl.when(owned(1 - core, t))(lambda: to_twin(t).wait_send())
        pl.when(owned(core, t))(lambda: pass_on(t).wait_send())

    def drain_peers(k):
        t = around(k)
        pl.when(owned(core, t))(lambda: to_owner(t).wait_send())
        pl.when(owned(core, chip))(lambda: spread(t).wait_send())

    def exchange(index):
        loop(1, start_twin)
        start_twin(0)
        loop(1, lambda k: reduce_pair(k, True))
        reduce_pair(0, False)

        @pl.when(owned(core, chip))
        def _():
            tile[...] = mine[chip]

            def gather(k):
                t = around(chips - k)
                from_peer(t).wait_recv()
                tile[...] += inbox[t]

            loop(1, gather)
            solved = []
            for b in range(PER):
                total = tile[9 * b : 9 * b + 9, :]
                total = jnp.where(index == 0, rhs[b] - total, total)
                piece = None
                for j in range(9):
                    term = inv[b, j] * total[j : j + 1, :]
                    piece = term if piece is None else piece + term
                solved.append(piece)
            solved = jnp.concatenate(solved + [jnp.zeros((ROWS - 9 * PER, 128), F32)], axis=0)
            step = kept[...] + solved
            kept[...] = step
            result[chunk(core, chip), :] = jnp.where(index == TERMS, step, solved)
            loop(1, lambda k: spread(around(k)).start())
            pass_on(chip).start()

        loop(1, forward)
        loop(0, finish)
        loop(0, drain)
        loop(1, drain_peers)

    def term(index, carry):
        solved = point_solve(pinv, zs[...])
        zs[...] = solved
        to_cameras(live, groups, zs, cj, pj, slot, point, hot, pull, x)
        exchange(index)
        zs[...] = to_points(live, groups, result, cj, pj, slot, point, quant, left, right)
        return carry

    lax.fori_loop(0, TERMS + 1, term, 0)
    rhs_pts = prhs[...]
    resid = rhs_pts - zs[...]
    for row, vals in ((0, resid * resid), (1, rhs_pts * rhs_pts)):
        total = vals[0:8]
        for k in range(1, 6):
            total = total + vals[8 * k : 8 * k + 8]
        tiles[8 * row : 8 * row + 8, :] = total

    def swap():
        return remote(tiles, pair, p_s, p_r, twin)

    def share(t, slot_of):
        return remote(left_tiles.at[chip], left_tiles.at[slot_of], q_s.at[t], q_r.at[slot_of], at(t))

    swap().start()
    swap().wait_recv()
    left_tiles[chip] = tiles[...] + pair[...]
    loop(1, lambda k: share(around(k), chip).start())
    zs[...] = point_solve(pinv, resid)
    for s in range(16):
        pt_out[:, s * 128 : s * 128 + 128] = zs[pl.ds(s, 3, stride=16), :]
    for b in range(blocks):
        base = (b // PER) * ROWS + (b % PER) * 9
        cam_out[:, b * 128 : b * 128 + 128] = result[base : base + 9, :]

    def collect(k):
        t = around(k)
        share(t, t).wait_recv()

    loop(1, collect)
    total = left_tiles[0]
    for t in range(1, chips):
        total = total + left_tiles[t]
    ratio_out[...] = jnp.sqrt(jnp.sum(total[0:8], keepdims=True) / jnp.sum(total[8:16], keepdims=True))
    loop(1, lambda k: share(around(k), chip).wait_send())
    swap().wait_send()


def local(pts_size, grp_size, cam_jac, pt_jac, cam_slot, obs_point, cam_inverse, pt_inverse, cam_rhs, pt_rhs):
    obs = cam_slot.shape[0]
    cameras = cam_rhs.shape[1]
    blocks = cameras // CAM_BLK
    points = pt_rhs.shape[1]
    chips = pts_size * grp_size // 2
    chunks = -(-blocks // PER)
    slots = -(-chunks // 16) * 8
    assert obs == blocks * 64 and slots <= chips and slots == 16 and points == 2048
    live = -(-obs // 128)
    groups = 2 * (-(-live // 16))

    def pad_obs(v):
        return jnp.pad(v, (0, 64 * 128 - obs)).reshape(64, 128)

    def vmem(*shape):
        return pltpu.VMEM(shape, F32)

    dma = pltpu.SemaphoreType.DMA
    anywhere = pl.BlockSpec(memory_space=pl.ANY)
    wide = live * 128
    camera_step, point_step, ratio = pl.pallas_call(
        functools.partial(body, chips, grp_size, chunks, slots, blocks, live, groups, obs),
        out_shape=(
            jax.ShapeDtypeStruct((9, cameras), F32),
            jax.ShapeDtypeStruct((3, points), F32),
            jax.ShapeDtypeStruct((1, 1), F32),
        ),
        in_specs=[VMEM] * 6 + [anywhere] * 2,
        out_specs=(VMEM, VMEM, VMEM),
        scratch_shapes=[
            vmem(18 * 64, 128), vmem(6 * 64, 128), vmem(9 * 16, 128), vmem(48, 128), vmem(16, 128),
            pltpu.VMEM((128, wide), BF16), pltpu.VMEM((128, wide), BF16), pltpu.VMEM((96, wide), BF16),
            vmem(3 * 64, 128), vmem(16 * 64, 128), vmem(48, 128), vmem(2 * slots * ROWS, 128),
            vmem(PER, 9, 9, 128), vmem(PER, 9, 128), vmem(ROWS, 128),
            vmem(slots, ROWS, 128), vmem(slots, ROWS, 128), vmem(chips, ROWS, 128), vmem(2 * slots * ROWS, 128),
            vmem(ROWS, 128), vmem(16, 128), vmem(16, 128), vmem(chips, 16, 128),
            dma((slots,)), dma((slots,)), dma((slots,)), dma((chips,)),
            dma((chips,)), dma((slots,)), dma((slots,)), dma((slots,)),
            dma((2 * PER,)), dma, dma, dma((chips,)), dma((chips,)),
        ],
        compiler_params=pltpu.CompilerParams(collective_id=0, has_side_effects=True),
        name="schur",
    )(cam_jac, pt_jac, pad_obs(cam_slot), pad_obs(obs_point), pt_inverse, pt_rhs, cam_inverse, cam_rhs)
    return camera_step, point_step, ratio.reshape(())


def solution(mesh):
    placed = (
        P(None, None, ("pts", "grp")),
        P(None, None, ("pts", "grp")),
        P(("pts", "grp")),
        P(("pts", "grp")),
        P(),
        P(None, None, ("pts", "grp")),
        P(),
        P(None, ("pts", "grp")),
    )
    return jax.shard_map(
        functools.partial(local, mesh.shape["pts"], mesh.shape["grp"]),
        mesh=mesh,
        in_specs=placed,
        out_specs=(P(), P(None, ("pts", "grp")), P()),
        check_vma=False,
    )
```

time: 929 us -> 115 us (0.12)
  waiting for transfers between devices: 520 us -> 0 us
  other arithmetic: 222 us -> 0 us
  Pallas kernels: 0 us -> 104 us
  local copies, waits for them, and re-layouts: 98 us -> 8.57 us
  blocking collectives: 40.1 us -> 0 us
  matrix products: 24.9 us -> 0 us
  between operations: 17.1 us -> 2.46 us
    psum x4 -> x0, waiting for transfers between devices: 520 us -> none  [combine(): summed = lax.psum(partial_sum, ('pts', 'grp'))]
    scatter-add x4 -> x0, other arithmetic: 159 us -> none  [to_points(): return jnp.zeros((3, points), jnp.float32).at[:, obs_point].add(lifted)]
    pallas_call x0 -> x1, Pallas kernels: none -> 104 us  [local(): pl.pallas_call(functools.partial(body, chips, grp_size, chunks, slots, bl...]
    gather x4 -> x0, local copies, waits for them, and re-layouts: 55.1 us -> none  [to_cameras(): at_obs = jnp.take(point_vec, obs_point, axis=1)]
    psum x1 -> x0, blocking collectives: 40.1 us -> none  [local(): lax.psum((jnp.sum(point_resid * point_resid), jnp.sum(pt_rhs * pt_rhs)),...]
    reduce_sum x26 -> x0, other arithmetic: 34.3 us -> none  [the longest x4 21.4 us: camera_solve(): return jnp.sum(inverse * camera_vec[None], axis=1)]
    select_n x5 -> x0, other arithmetic: 25.6 us -> none  [to_cameras(): at_obs = jnp.take(point_vec, obs_point, axis=1)]
    dot_general x8 -> x0, matrix products: 24.9 us -> none  [the longest x4 14 us: fetch_cams(): jnp.einsum('cbk,bsk->cbs', grouped, picker, precision=lax.Precision.HIGHEST)]
  transfers between devices with their start and end apart: 4 -> 0, of which waited for: 4 -> 0; matrix products, arithmetic and copies ran while one was open for 0% -> 0% of each run, Pallas kernels for 0% -> 0%
where the time goes in v2:
time: 115 us
  Pallas kernels  104 us (90%)
  local copies, waits for them, and re-layouts  8.57 us (7%)
  between operations  2.46 us (2%)
    pallas_call x1, Pallas kernels, local(): pl.pallas_call(functools.partial(body, chips, grp_size, chunks, slots, bl...  104 us
    unnamed x4, local copies, waits for them, and re-layouts  7.19 us

profile of v2, /device:TPU:0, one launch (start us, length us, event | category | flops | bytes accessed | tf_op | source)
XLA Modules:
  0.0 115.0 jit_solution(6004354108646725576)
XLA Ops:
  0.6 1.4 %pad_bitcast_fusion = (s32[64,128]{1,0:T(8,128)}, s32[64,128]{1,0:T(8,128)}) fusion(s32[6848]{0:T(1024)} %param.11, s32[6848]{0:T(1024)} %param.10), kind=kLoop, calls=%fused_computation | loop fusion | bytes 120320 | tf_op jit(solution)/shard_map/reshape | solution.py:374
  2.0 1.7 %copy.12.pj_in = f32[2,3,6848]{2,1,0:T(4,128)} copy(f32[2,3,6848]{2,0,1:T(2,128)} %param.9) | data formatting | bytes 328704 | tf_op args[1]
  3.7 2.0 %copy.11.cj_in = f32[2,9,6848]{2,1,0:T(8,128)} copy(f32[2,9,6848]{2,0,1:T(2,128)} %param.8) | data formatting | bytes 986112 | tf_op args[0]
  5.7 104.0 %schur.1 = (f32[9,13696]{1,0:T(8,128)}, f32[3,2048]{1,0:T(4,128)}, f32[1,1]{1,0:T(1,128)}) custom-call(f32[2,9,6848]{2,1,0:T(8,128)} %copy.11.cj_in, f32[2,3,6848]{2,1,0:T(4,128)} %copy.12.pj_in, s32[64,128]{1,0:T(8,128)} %get-tuple-element.10.slot, s32[64,128]{1,0:T(8,128)} %get-tuple-element.9.point, f32[3,3,2048]{2,1,0:T(4,128)} %pinv_in.1, ...), custom_call_target="tpu_custom_call" | custom-call | tf_op jit(solution)/shard_map/schur/pallas_call | solution.py:382
  109.7 2.1 %copy.16 = f32[9,13696]{1,0:T(8,128)} copy(f32[9,13696]{1,0:T(8,128)} %get-tuple-element.14) | data formatting | bytes 986112
  111.8 1.4 %copy.17 = f32[3,2048]{1,0:T(4,128)} copy(f32[3,2048]{1,0:T(4,128)} %get-tuple-element.15) | data formatting | bytes 49152

commit v3 on v2

--- a/solution.py
+++ b/solution.py
@@ -26,23 +26,26 @@
     return 16 * (group // 2) + group % 2
 
 
-def prepare(obs, live, cj_in, pj_in, slot, point, pinv_in, prhs_in, cj, pj, pinv, prhs, tail, right, hot):
-    for a in range(2):
-        for ref, out, count in ((cj_in, cj, 9), (pj_in, pj, 3)):
-            for j in range(count):
-                begin = live // 8 * 8
-                out[(a * count + j) * 64 + begin : (a * count + j + 1) * 64, :] = jnp.zeros((64 - begin, 128), F32)
+def prepare(
+    obs, live, cj_in, pj_in, slot_in, point_in, pinv_in, prhs_in, cj, pj, slot, point, pinv, prhs, tail, right, hot
+):
+    begin = live // 8 * 8
+    for ref, count in ((cj, 18), (pj, 6), (slot, 1), (point, 1)):
+        for j in range(count):
+            ref[j * 64 + begin : (j + 1) * 64, :] = jnp.zeros((64 - begin, 128), ref.dtype)
     tail[...] = jnp.zeros((16, 128), F32)
     for r in range(live):
         span = min(128, obs - r * 128)
-        for a in range(2):
-            for ref, out, count in ((cj_in, cj, 9), (pj_in, pj, 3)):
-                if span == 128:
-                    v = ref[a, :, r * 128 : r * 128 + 128]
-                else:
-                    tail[0:count, 0:span] = ref[a, :, r * 128 : r * 128 + span]
-                    v = tail[0:count, :]
-                out[pl.ds(a * count * 64 + r, count, stride=64), :] = v
+        cols = slice(r * 128, r * 128 + span)
+        for ref, out, count in ((cj_in, cj, 9), (pj_in, pj, 3)):
+            for j in range(count):
+                v = ref[j, :, cols]
+                if span < 128:
+                    tail[0:2, 0:span] = v
+                    v = tail[0:2, :]
+                out[pl.ds(j * 64 + r, 2, stride=count * 64), :] = v
+        slot[r : r + 1, 0:span] = slot_in[0:1, cols]
+        point[r : r + 1, 0:span] = point_in[0:1, cols]
     for s in range(16):
         cols = slice(s * 128, s * 128 + 128)
         prhs[pl.ds(s, 3, stride=16), :] = prhs_in[:, cols]
@@ -99,7 +102,7 @@
     return jnp.concatenate(out, axis=0)
 
 
-def to_cameras(live, groups, z, cj, pj, slot, point, hot, pull, out):
+def pull_back(groups, z, cj, pj, point, pull):
     for group in range(groups):
         row = rows_of(group)
         where = point[pl.ds(row, 8, stride=2), :]
@@ -123,8 +126,11 @@
                 cj[pl.ds(64 * j + row, 8, stride=2), :] * proj[0]
                 + cj[pl.ds(64 * (9 + j) + row, 8, stride=2), :] * proj[1]
             )
+
+
+def deposit(rows, hot, pull, out):
     lane_low = lax.broadcasted_iota(jnp.int32, (16, 128), 1) < 64
-    for r in range(live):
+    for r in rows:
         v = pull[pl.ds(r, 16, stride=64), :]
         e_top, e_rest = halves(jnp.where(lane_low, v, 0.0))
         o_top, o_rest = halves(jnp.where(lane_low, 0.0, v))
@@ -139,9 +145,9 @@
 
 def body(
     chips, grp_size, chunks, slots, blocks, live, groups, obs,
-    cj_in, pj_in, slot, point, pinv_in, prhs_in, cinv, crhs,
+    cj_in, pj_in, slot_in, point_in, pinv_in, prhs_in, cinv, crhs,
     cam_out, pt_out, ratio_out,
-    cj, pj, pinv, prhs, tail, right, hot, left, quant, pull, zs, x, inv, rhs, kept,
+    cj, pj, slot, point, pinv, prhs, tail, right, hot, left, quant, pull, zs, x, inv, rhs, kept,
     twin_buf, mine, inbox, result, tile, pair, tiles, left_tiles,
     a_s, a_r, b_s, b_r, c_s, c_r, d_s, d_r, load, p_s, p_r, q_s, q_r,
 ):
@@ -167,14 +173,17 @@
     pl.semaphore_signal(barrier, inc=1, device_id=twin, device_id_type=MESH)
     loop(1, lambda k: pl.semaphore_signal(barrier, inc=1, device_id=at(around(k)), device_id_type=MESH))
 
+    def number(c, t):
+        return 2 * lax.rem(13 * t, slots) + c
+
     def owned(c, t):
-        return jnp.logical_and(t < slots, c * slots + t < chunks)
+        return jnp.logical_and(t < slots, number(c, t) < chunks)
 
     def owned_block(b):
-        return jnp.logical_and(chip < slots, (core * slots + chip) * PER + b < blocks)
+        return jnp.logical_and(chip < slots, number(core, chip) * PER + b < blocks)
 
     def loads(b):
-        cols = pl.ds(pl.multiple_of(((core * slots + chip) * PER + b) * 128, 128), 128)
+        cols = pl.ds(pl.multiple_of((number(core, chip) * PER + b) * 128, 128), 128)
         return (
             pltpu.make_async_copy(cinv.at[:, :, cols], inv.at[b], load.at[2 * b]),
             pltpu.make_async_copy(crhs.at[:, cols], rhs.at[b], load.at[2 * b + 1]),
@@ -191,7 +200,10 @@
             inv[b] = jnp.zeros((9, 9, 128), F32)
             rhs[b] = jnp.zeros((9, 128), F32)
 
-    prepare(obs, live, cj_in, pj_in, slot, point, pinv_in, prhs_in, cj, pj, pinv, prhs, tail, right, hot)
+    prepare(
+        obs, live, cj_in, pj_in, slot_in, point_in, pinv_in, prhs_in,
+        cj, pj, slot, point, pinv, prhs, tail, right, hot,
+    )
     x[...] = jnp.zeros_like(x)
     result[...] = jnp.zeros_like(result)
     kept[...] = jnp.zeros_like(kept)
@@ -206,7 +218,7 @@
     pl.semaphore_wait(barrier, chips)
 
     def chunk(c, t):
-        return pl.ds(pl.multiple_of((c * slots + t) * ROWS, 8), ROWS)
+        return pl.ds(pl.multiple_of(number(c, t) * ROWS, 8), ROWS)
 
     def remote(src, dst, send, recv, device):
         return pltpu.make_async_remote_copy(
@@ -238,14 +250,20 @@
         part = result.at[chunk(1 - core, t)]
         return remote(part, part, d_s.at[0], d_r.at[t], twin)
 
-    def start_twin(k):
-        t = around(k)
-        pl.when(owned(1 - core, t))(lambda: to_twin(t).start())
-
-    def reduce_pair(k, send):
-        t = around(k)
-
-        @pl.when(owned(core, t))
+    early = -(-chunks // 4)
+
+    def within(c, t, part):
+        first = number(c, t) < 2 * early
+        return jnp.logical_and(owned(c, t), first if part == 0 else jnp.logical_not(first))
+
+    def start_twin(k, part):
+        t = around(k)
+        pl.when(within(1 - core, t, part))(lambda: to_twin(t).start())
+
+    def reduce_pair(k, send, part):
+        t = around(k)
+
+        @pl.when(within(core, t, part))
         def _():
             to_twin(t).wait_recv()
             mine[t] = x[chunk(core, t), :] + twin_buf[t]
@@ -275,10 +293,10 @@
         pl.when(owned(core, chip))(lambda: spread(t).wait_send())
 
     def exchange(index):
-        loop(1, start_twin)
-        start_twin(0)
-        loop(1, lambda k: reduce_pair(k, True))
-        reduce_pair(0, False)
+        for part in range(2):
+            loop(1, lambda k: reduce_pair(k, True, part))
+        for part in range(2):
+            reduce_pair(0, False, part)
 
         @pl.when(owned(core, chip))
         def _():
@@ -314,7 +332,13 @@
     def term(index, carry):
         solved = point_solve(pinv, zs[...])
         zs[...] = solved
-        to_cameras(live, groups, zs, cj, pj, slot, point, hot, pull, x)
+        pull_back(groups, zs, cj, pj, point, pull)
+        deposit(range(4 * early), hot, pull, x)
+        loop(1, lambda k: start_twin(k, 0))
+        start_twin(0, 0)
+        deposit(range(4 * early, live), hot, pull, x)
+        loop(1, lambda k: start_twin(k, 1))
+        start_twin(0, 1)
         exchange(index)
         zs[...] = to_points(live, groups, result, cj, pj, slot, point, quant, left, right)
         return carry
@@ -369,9 +393,6 @@
     assert obs == blocks * 64 and slots <= chips and slots == 16 and points == 2048
     live = -(-obs // 128)
     groups = 2 * (-(-live // 16))
-
-    def pad_obs(v):
-        return jnp.pad(v, (0, 64 * 128 - obs)).reshape(64, 128)
 
     def vmem(*shape):
         return pltpu.VMEM(shape, F32)
@@ -389,7 +410,8 @@
         in_specs=[VMEM] * 6 + [anywhere] * 2,
         out_specs=(VMEM, VMEM, VMEM),
         scratch_shapes=[
-            vmem(18 * 64, 128), vmem(6 * 64, 128), vmem(9 * 16, 128), vmem(48, 128), vmem(16, 128),
+            vmem(18 * 64, 128), vmem(6 * 64, 128),
+            pltpu.VMEM((64, 128), jnp.int32), pltpu.VMEM((64, 128), jnp.int32), vmem(9 * 16, 128), vmem(48, 128), vmem(16, 128),
             pltpu.VMEM((128, wide), BF16), pltpu.VMEM((128, wide), BF16), pltpu.VMEM((96, wide), BF16),
             vmem(3 * 64, 128), vmem(16 * 64, 128), vmem(48, 128), vmem(2 * slots * ROWS, 128),
             vmem(PER, 9, 9, 128), vmem(PER, 9, 128), vmem(ROWS, 128),
@@ -401,7 +423,10 @@
         ],
         compiler_params=pltpu.CompilerParams(collective_id=0, has_side_effects=True),
         name="schur",
-    )(cam_jac, pt_jac, pad_obs(cam_slot), pad_obs(obs_point), pt_inverse, pt_rhs, cam_inverse, cam_rhs)
+    )(
+        jnp.transpose(cam_jac, (1, 0, 2)), jnp.transpose(pt_jac, (1, 0, 2)),
+        cam_slot.reshape(1, obs), obs_point.reshape(1, obs), pt_inverse, pt_rhs, cam_inverse, cam_rhs,
+    )
     return camera_step, point_step, ratio.reshape(())
 
 

time: 115 us -> 116 us (level)
  Pallas kernels: 104 us -> 107 us
  local copies, waits for them, and re-layouts: 8.57 us -> 6.26 us
    unnamed x4 -> x2, local copies, waits for them, and re-layouts: 7.19 us -> 3.51 us
    pallas_call x1, Pallas kernels: 104 us -> 107 us  [local(): pl.pallas_call(functools.partial(body, chips, grp_size, chunks, slots, bl...]
    reshape x1 -> x2, local copies, waits for them, and re-layouts: 1.39 us -> 2.75 us  [the longest x1 1.38 us: local(): cam_slot.reshape(1, obs)]
where the time goes in v3:
time: 116 us; the launch traced here: 115 us
  Pallas kernels  107 us (92%)
  local copies, waits for them, and re-layouts  6.26 us (5%)
  between operations  2.44 us (2%)
    pallas_call x1, Pallas kernels, local(): pl.pallas_call(functools.partial(body, chips, grp_size, chunks, slots, bl...  107 us
    unnamed x2, local copies, waits for them, and re-layouts  3.51 us

profile of v3, /device:TPU:0, one launch (start us, length us, event | category | flops | bytes accessed | tf_op | source)
XLA Modules:
  0.0 115.5 jit_solution(3229846561281992281)
XLA Ops:
  0.6 1.4 %reshape.15.slot_in = s32[1,6848]{1,0:T(1,128)} reshape(s32[6848]{0:T(1024)} %param.10) | data formatting | bytes 54784 | tf_op jit(solution)/shard_map/reshape | solution.py:428
  2.0 1.4 %reshape.16.point_in = s32[1,6848]{1,0:T(1,128)} reshape(s32[6848]{0:T(1024)} %param.11) | data formatting | bytes 54784 | tf_op jit(solution)/shard_map/reshape | solution.py:428
  3.4 106.8 %schur.1 = (f32[9,13696]{1,0:T(8,128)}, f32[3,2048]{1,0:T(4,128)}, f32[1,1]{1,0:T(1,128)}) custom-call(f32[9,2,6848]{2,1,0:T(2,128)} %bitcast.3, f32[3,2,6848]{2,1,0:T(2,128)} %bitcast.4, s32[1,6848]{1,0:T(1,128)} %reshape.15.slot_in, s32[1,6848]{1,0:T(1,128)} %reshape.16.point_in, f32[3,3,2048]{2,1,0:T(4,128)} %pinv_in.1, f32[3,2048]{1,0:T(4,128)} %prhs_in.1, ...), custom_call_target="tpu_custom_call" | custom-call | tf_op jit(solution)/shard_map/schur/pallas_call | solution.py:403
  110.2 2.1 %copy.14 = f32[9,13696]{1,0:T(8,128)} copy(f32[9,13696]{1,0:T(8,128)} %get-tuple-element.12) | data formatting | bytes 986112
  112.3 1.4 %copy.15 = f32[3,2048]{1,0:T(4,128)} copy(f32[3,2048]{1,0:T(4,128)} %get-tuple-element.13) | data formatting | bytes 49152
